TPU v7x, 256 devices: a whole 4x4x8 slice. The times are simulated.
256 devices in a mesh: toa: 128 (over z, y, x), rep: 2 (over core).
Axes of the slice: x: 4, y: 4, z: 8, core: 2. Of those that a mesh axis runs over, the one named last changes fastest.
Arguments:
- residual: float32 [16384, 256], P('toa'), may hold values from -6 to 6
- toa_error: float32 [16384, 256], P('toa'), may hold values from 0.3 to 3
- basis_rows: bfloat16 [16384, 100, 256], P('toa', 'rep'), may hold values from -0.041432038 to 0.041432038
- efac_table: float32 [128, 64], replicated, may hold values from 0.5 to 2
- equad_table: float32 [128, 64], replicated, may hold values from 0.1 to 1
- pulsar: int32 [16384], P('toa'), may hold values from 0 to 127
- backend: int32 [16384], P('toa'), may hold values from 0 to 63
- counts: int32 [16384], P('toa'), may hold values from 64 to 256
- owner_slot: int32 [16384], P('toa'), may hold values from 0 to 16383, as said below
Outputs:
- gram_matrix: float32 [128, 100, 100], P('toa', None, 'rep')
- projection: float32 [128, 100], P('toa', 'rep')
- whitened: float32 [16384, 256], P('toa')
Inputs may be any that keep to these rules, and one draw needn't show every extreme that they name: A permutation of the 16384 slots, independent of pulsar and backend; owner_slot // 128 is the device index along toa that holds the tile's output row and owner_slot % 128 its place there; each device's tiles go exactly 1 to each device.
All inputs are finite; a program needn't handle non-finite values.
Results may differ from a plain program's by a relative error of at most 0.0032.
Values may be sent and summed in bfloat16 or wider, within the bound.
No kernel may reach another device: no remote copies, remote signals or barrier semaphores. Data moves between devices by JAX's collectives and lax.ppermute only.
A program may use at most 64 MiB of HBM per device.

v0:
```python
import jax
import jax.numpy as jnp
from jax import lax
from jax.sharding import Mesh
from jax.sharding import PartitionSpec as P

TOA = ("toa_0", "toa_1", "toa_2")


def in_blocks(value, dim, peers):
    shape = value.shape
    pieces = value.reshape(*shape[:dim], peers, shape[dim] // peers, *shape[dim + 1 :])
    return jnp.moveaxis(pieces, dim, 0)


def sum_at_owner(value, axis, dim):
    peers = lax.axis_size(axis)
    pieces = lax.all_to_all(in_blocks(value, dim, peers), axis, 0, 0, tiled=True)
    return jnp.sum(pieces, axis=0)


def summed_rows(value, axes, dim):
    far, near = axes
    own = sum_at_owner(in_blocks(value, dim, lax.axis_size(far)), near, dim + 1)
    return jnp.sum(lax.all_to_all(own, far, 0, 0, tiled=True), axis=0)


def side_by_side(arrays, axis, dim, along):
    columns = [a.reshape(*a.shape[:along], -1) for a in arrays]
    both = jnp.concatenate(columns, axis=along)
    filled, at, done = (summed_rows(both, axis, dim), 0, [])
    for a, column in zip(arrays, columns):
        section = filled[..., at : at + column.shape[along]]
        done.append(section.reshape(*section.shape[:along], *a.shape[along:]))
        at += column.shape[along]
    return tuple(done)


def sent_together(arrays, axis, split_dim, concat_dim, along):
    ends, at = ([], 0)
    for a in arrays[:-1]:
        at += a.shape[along]
        ends.append(at)
    both = jnp.concatenate(arrays, axis=along)
    return tuple(
        jnp.split(
            lax.all_to_all(both, axis, split_axis=split_dim, concat_axis=concat_dim, tiled=True),
            ends,
            axis=along,
        )
    )


def lookup(small_table, onehot_pulsar, onehot_backend):
    table_rows = jnp.dot(onehot_pulsar, small_table, precision=lax.Precision.HIGHEST)
    return jnp.sum(table_rows * onehot_backend, axis=1)


def tile_weights(residual, toa_error, pulsar, backend, counts, efac_table, equad_table):
    onehot_pulsar = (
        pulsar[:, None] == jnp.arange(efac_table.shape[0], dtype=jnp.int32)[None, :]
    ).astype(jnp.float32)
    onehot_backend = (
        backend[:, None] == jnp.arange(efac_table.shape[1], dtype=jnp.int32)[None, :]
    ).astype(jnp.float32)
    factor = lookup(efac_table, onehot_pulsar, onehot_backend)
    floor_term = lookup(equad_table, onehot_pulsar, onehot_backend)
    valid_rows = jnp.arange(residual.shape[1], dtype=jnp.int32)[None, :] < counts[:, None]
    weight = jnp.where(
        valid_rows, 1.0 / (factor[:, None] ** 2 * toa_error**2 + floor_term[:, None] ** 2), 0.0
    )
    return (onehot_pulsar, weight)


def pulsar_terms(basis_own, weight, residual, onehot_pulsar):
    scaled = (weight[:, None, :] * basis_own).astype(jnp.bfloat16)
    weighted_res = (weight * residual).astype(jnp.bfloat16)
    tile_gram = jnp.einsum(
        "tkr,tjr->tkj",
        lax.all_gather(basis_own, "rep", axis=1, tiled=True),
        scaled,
        preferred_element_type=jnp.float32,
    )
    tile_proj = jnp.einsum(
        "tjr,tr->tj", basis_own, weighted_res, preferred_element_type=jnp.float32
    )
    tile_total, full_width, half_width = tile_gram.shape
    pulsar_total = onehot_pulsar.shape[1]
    gram_part = jnp.dot(
        onehot_pulsar.T,
        tile_gram.reshape(tile_total, full_width * half_width),
        precision=lax.Precision.HIGHEST,
    )
    gram_part = gram_part.reshape(pulsar_total, full_width, half_width)
    proj_part = jnp.dot(onehot_pulsar.T, tile_proj, precision=lax.Precision.HIGHEST)
    return side_by_side((gram_part, proj_part), ("toa_0", ("toa_1", "toa_2")), 0, 1)


def shards(
    residual, toa_error, basis_rows, efac_table, equad_table, pulsar, backend, counts, owner_slot
):
    tile_count = residual.shape[0]
    peer_count = lax.axis_size(TOA)
    per_peer = tile_count // peer_count
    owner_dev = owner_slot // tile_count
    owner_place = owner_slot % tile_count
    onehot_dest = (owner_dev[:, None] == jnp.arange(peer_count, dtype=jnp.int32)[None, :]).astype(
        jnp.int32
    )
    bucket_rank = jnp.sum((jnp.cumsum(onehot_dest, axis=0) - 1) * onehot_dest, axis=1)
    send_position = owner_dev * per_peer + bucket_rank
    send_order = (
        jnp.zeros((tile_count,), jnp.int32)
        .at[send_position]
        .set(jnp.arange(tile_count, dtype=jnp.int32))
    )
    onehot_pulsar, weight = tile_weights(
        residual, toa_error, pulsar, backend, counts, efac_table, equad_table
    )
    whitened_local = jnp.sqrt(weight) * residual
    place_float = owner_place[send_order][:, None].astype(jnp.float32)
    moved_white, moved_place = sent_together(
        (whitened_local[send_order], place_float), TOA, 0, 0, 1
    )
    whitened = jnp.zeros_like(moved_white).at[moved_place[:, 0].astype(jnp.int32)].set(moved_white)
    gram_matrix, projection = pulsar_terms(basis_rows, weight, residual, onehot_pulsar)
    return (gram_matrix, projection, whitened)


def solution(mesh):
    split = Mesh(
        mesh.devices.reshape(8, 4, 4, mesh.shape["rep"]), ("toa_0", "toa_1", "toa_2", "rep")
    )
    placed = (
        P(TOA, None),
        P(TOA, None),
        P(TOA, "rep", None),
        P(),
        P(),
        P(TOA),
        P(TOA),
        P(TOA),
        P(TOA),
    )
    return jax.shard_map(
        shards,
        mesh=split,
        in_specs=placed,
        out_specs=(P(TOA, None, "rep"), P(TOA, "rep"), P(TOA, None)),
        check_vma=False,
    )
```

profile of v0, /device:TPU:2, one launch (start us, length us, event | category | flops | bytes accessed | tf_op | source)
XLA Modules:
  0.0 154.6 jit_solution(5533874653531388217)
XLA Ops:
  8.6 1.6 %sqrt_multiply_fusion = (f32[128,256]{1,0:T(8,128)S(1)}, f32[128,256]{1,0:T(8,128)S(1)}) fusion(f32[128,256]{1,0:T(8,128)} %param.9, f32[128]{0:T(128)S(1)} %integer_pow.21, f32[128,256]{1,0:T(8,128)} %param.10, f32[128]{0:T(128)S(1)} %integer_pow.19, s32[128]{0:T(128)S(1)} %copy-done.3), kind=kLoop, calls=%fused_computation.21 | loop fusion | flops 229376 | bytes 525824 | tf_op jit(solution)/shard_map/mul | solution.py:120
  10.2 0.9 fusion.15
  11.2 1.9 %fusion.2 = f32[128,1,50]{2,1,0:T(1,128)S(1)} fusion(bf16[128,50,256]{2,0,1:T(8,128)(2,1)S(1)} %copy-done.1, bf16[128,256,1]{1,0,2:T(8,128)(2,1)S(1)} %fusion.15), kind=kOutput, calls=%fused_computation.7 | convolution fusion | flops 3276800 | bytes 3367936 | tf_op jit(solution)/shard_map/tjr,tr->tj/dot_general | solution.py:84
  13.3 1.0 multiply_convert_fusion
  14.3 21.0 %all-gather.2.cloned.1.call-done = bf16[128,100,256]{2,0,1:T(8,128)(2,1)} async-done(((bf16[128,50,256]{2,0,1:T(8,128)(2,1)}), bf16[128,100,256]{2,0,1:T(8,128)(2,1)}) %all-gather.2.cloned.1.call-update) | async-done | bytes 6553616 | tf_op jit(solution)/shard_map/all_gather | solution.py:80
  35.3 10.3 %fusion.5 = f32[128,100,50]{1,2,0:T(8,128)} fusion(bf16[128,100,256]{2,0,1:T(8,128)(2,1)} %all-gather.2.cloned.1.call-done, bf16[128,50,256]{2,0,1:T(8,128)(2,1)S(1)} %multiply_convert_fusion), kind=kOutput, calls=%fused_computation.11 | convolution fusion | flops 327680000 | bytes 12390400 | tf_op jit(solution)/shard_map/tkr,tjr->tkj/dot_general | solution.py:78
  45.6 3.7 %copy.31 = f32[128,100,50]{0,2,1:T(8,128)S(1)} copy(f32[128,100,50]{1,2,0:T(8,128)} %fusion.5) | data formatting | bytes 5120000 | tf_op jit(solution)/shard_map/tkr,tjr->tkj/dot_general | solution.py:78
  49.3 1.7 %reshape.38 = f32[128,5000]{0,1:T(8,128)} reshape(f32[128,100,50]{0,2,1:T(8,128)S(1)} %copy.31) | data formatting | bytes 5120000 | tf_op jit(solution)/shard_map/reshape | solution.py:91
  50.9 4.0 %fusion.19 = f32[128,5000]{0,1:T(8,128)S(1)} fusion(f32[128,5000]{0,1:T(8,128)} %reshape.38, s32[128]{0:T(128)S(1)} %copy-done.4), kind=kOutput, calls=%fused_computation.32 | convolution fusion | flops 983056384 | bytes 5120512 | tf_op jit(solution)/shard_map/dot_general | solution.py:89
  54.9 1.7 %pad_maximum_fusion = f32[128,5050]{0,1:T(8,128)} fusion(f32[128,50]{0,1:T(8,128)S(1)} %fusion.18, f32[128,5000]{0,1:T(8,128)S(1)} %fusion.19), kind=kLoop, calls=%fused_computation.10 | loop fusion | flops 646400 | bytes 5171200 | tf_op jit(solution)/shard_map/concatenate | solution.py:30
  56.6 2.1 %copy.32 = f32[128,5050]{1,0:T(8,128)S(1)} copy(f32[128,5050]{0,1:T(8,128)} %pad_maximum_fusion) | data formatting | bytes 5171200 | tf_op jit(solution)/shard_map/concatenate | solution.py:30
  58.7 3.0 %copy.33 = f32[16,8,1,5050]{3,1,2,0:T(8,128)} copy(f32[16,8,1,5050]{3,0,1,2:T(8,128)S(1)} %bitcast.28) | data formatting | bytes 5171200 | tf_op jit(solution)/shard_map/transpose | solution.py:13
  61.8 7.4 %all-to-all-start = ((f32[16,8,1,5050]{3,1,2,0:T(8,128)}), f32[16,8,1,5050]{3,1,2,0:T(8,128)S(1)}, u32[]{:S(2)}, u32[]{:S(2)}) async-start(f32[16,8,1,5050]{3,1,2,0:T(8,128)} %copy.33), calls=%async_computation | async-start | bytes 5242880 | tf_op jit(solution)/shard_map/all_to_all | solution.py:18
  69.7 1.0 scatter_custom_fusion
  70.7 1.2 gather_fusion.1
  72.0 0.8 gather_fusion
  72.8 0.9 copy.35
  73.7 32.2 %all-to-all-done = f32[16,8,1,5050]{3,1,2,0:T(8,128)S(1)} async-done(((f32[16,8,1,5050]{3,1,2,0:T(8,128)}), f32[16,8,1,5050]{3,1,2,0:T(8,128)S(1)}, u32[]{:S(2)}, u32[]{:S(2)}) %all-to-all-start) | async-done | bytes 2585632 | tf_op jit(solution)/shard_map/all_to_all | solution.py:18
  105.9 15.0 %all-to-all-start.2 = ((f32[128,1,257]{2,1,0:T(1,128)}), f32[128,1,257]{2,1,0:T(1,128)S(1)}, u32[]{:S(2)}, u32[]{:S(2)}) async-start(f32[128,1,257]{2,1,0:T(1,128)} %copy.35), calls=%async_computation.2 | async-start | bytes 393216 | tf_op jit(solution)/shard_map/all_to_all | solution.py:47
  121.0 0.8 reduce_sum.52
  121.8 11.6 %all-to-all-done.2 = f32[128,1,257]{2,1,0:T(1,128)S(1)} async-done(((f32[128,1,257]{2,1,0:T(1,128)}), f32[128,1,257]{2,1,0:T(1,128)S(1)}, u32[]{:S(2)}, u32[]{:S(2)}) %all-to-all-start.2) | async-done | bytes 131616 | tf_op jit(solution)/shard_map/all_to_all | solution.py:47
  133.4 3.4 %all-to-all-start.1 = ((f32[8,1,5050]{2,1,0:T(1,128)}), f32[8,1,5050]{2,1,0:T(1,128)S(1)}, u32[]{:S(2)}, u32[]{:S(2)}) async-start(f32[8,1,5050]{2,1,0:T(1,128)} %reduce_sum.52), calls=%async_computation.1 | async-start | bytes 327680 | tf_op jit(solution)/shard_map/all_to_all | solution.py:25
  137.0 1.6 %scatter_custom_fusion.1 = f32[128,256]{1,0:T(8,128)} fusion(s32[128]{0:T(128)S(1)} %fusion.24, f32[128,257]{1,0:T(8,128)S(1)} %bitcast.29, f32[]{:T(128)} %constant.37.clone.1), kind=kCustom, calls=%fused_computation.18 | custom fusion | bytes 262148 | tf_op jit(solution)/shard_map/scatter | solution.py:125
  138.6 7.6 %all-to-all-done.1 = f32[8,1,5050]{2,1,0:T(1,128)S(1)} async-done(((f32[8,1,5050]{2,1,0:T(1,128)}), f32[8,1,5050]{2,1,0:T(1,128)S(1)}, u32[]{:S(2)}, u32[]{:S(2)}) %all-to-all-start.1) | async-done | bytes 161632 | tf_op jit(solution)/shard_map/all_to_all | solution.py:25
  (43 shorter events, 4.1 us)
Async XLA Ops:
  7.2 0.8 copy-start
  7.2 4.0 %copy-start.1 = (bf16[128,50,256]{2,0,1:T(8,128)(2,1)S(1)}, bf16[128,50,256]{2,0,1:T(8,128)(2,1)}, u32[]{:S(2)}) copy-start(bf16[128,50,256]{2,0,1:T(8,128)(2,1)} %param.11) | copy-start | bytes 9830404
  7.2 0.8 copy-start.4
  7.2 0.8 copy-start.6
  7.2 1.1 copy-start.5
  7.2 1.4 copy-start.3
  7.2 28.1 %all-gather.2.cloned.1.call-start = ((), (), s32[]{:S(2)}) async-start(), calls=%async_computation.3 | async-start | bytes 9830400 | tf_op jit(solution)/shard_map/all_gather | solution.py:80
  8.0 5.3 %copy-start.2 = (bf16[128,50,256]{2,0,1:T(8,128)(2,1)S(1)}, bf16[128,50,256]{2,0,1:T(8,128)(2,1)}, u32[]{:S(2)}) copy-start(bf16[128,50,256]{2,0,1:T(8,128)(2,1)} %param.11) | copy-start | bytes 9830404
  61.8 7.4 %copy-start.7 = (s32[128]{0:T(128)S(1)}, s32[128]{0:T(128)}, u32[]{:S(2)}) copy-start(s32[128]{0:T(128)} %param.17) | copy-start | bytes 1540
  61.8 44.1 %all-to-all-start = ((f32[16,8,1,5050]{3,1,2,0:T(8,128)}), f32[16,8,1,5050]{3,1,2,0:T(8,128)S(1)}, u32[]{:S(2)}, u32[]{:S(2)}) async-start(f32[16,8,1,5050]{3,1,2,0:T(8,128)} %copy.33), calls=%async_computation | async-start | bytes 5242880 | tf_op jit(solution)/shard_map/all_to_all | solution.py:18
  105.9 27.5 %all-to-all-start.2 = ((f32[128,1,257]{2,1,0:T(1,128)}), f32[128,1,257]{2,1,0:T(1,128)S(1)}, u32[]{:S(2)}, u32[]{:S(2)}) async-start(f32[128,1,257]{2,1,0:T(1,128)} %copy.35), calls=%async_computation.2 | async-start | bytes 393216 | tf_op jit(solution)/shard_map/all_to_all | solution.py:47
  133.4 12.7 %all-to-all-start.1 = ((f32[8,1,5050]{2,1,0:T(1,128)}), f32[8,1,5050]{2,1,0:T(1,128)S(1)}, u32[]{:S(2)}, u32[]{:S(2)}) async-start(f32[8,1,5050]{2,1,0:T(1,128)} %reduce_sum.52), calls=%async_computation.1 | async-start | bytes 327680 | tf_op jit(solution)/shard_map/all_to_all | solution.py:25
Sparse Core Ops, SparseCore 0:
  9.8 25.4 all-gather.1
where the time goes:
time: 155 us
  waiting for transfers between devices  73.1 us (47%)
  starting transfers between devices  25.8 us (17%)
  local copies, waits for them, and re-layouts  18.5 us (12%)
  matrix products  17 us (11%)
  between operations  14.3 us (9%)
  other arithmetic  5.89 us (4%)
    all_to_all x1, waiting for transfers between devices, sum_at_owner(): lax.all_to_all(in_blocks(value, dim, peers), axis, 0, 0, tiled=True)  32.2 us
    all_gather x1, waiting for transfers between devices, pulsar_terms(): lax.all_gather(basis_own, 'rep', axis=1, tiled=True)  21 us
    all_to_all x1, starting transfers between devices, sent_together(): lax.all_to_all(both, axis, split_axis=split_dim, concat_axis=concat_dim,...  15 us
    all_to_all x1, waiting for transfers between devices, sent_together(): lax.all_to_all(both, axis, split_axis=split_dim, concat_axis=concat_dim,...  11.6 us
    dot_general x1, matrix products, pulsar_terms(): jnp.einsum('tkr,tjr->tkj', lax.all_gather(basis_own, 'rep', axis=1, tiled...  10.3 us
    all_to_all x1, waiting for transfers between devices, summed_rows(): return jnp.sum(lax.all_to_all(own, far, 0, 0, tiled=True), axis=0)  7.56 us
    all_to_all x1, starting transfers between devices, sum_at_owner(): lax.all_to_all(in_blocks(value, dim, peers), axis, 0, 0, tiled=True)  7.4 us
    dot_general x1, matrix products, pulsar_terms(): jnp.dot(onehot_pulsar.T, tile_gram.reshape(tile_total, full_width * half_...  4 us
  transfers between devices with their start and end apart: 4, of which 4 were waited for; matrix products, arithmetic and copies ran while one was open for 9% of the time, Pallas kernels for 0%

commit v1 on v0

--- a/solution.py
+++ b/solution.py
@@ -5,6 +5,14 @@
 from jax.sharding import PartitionSpec as P
 
 TOA = ("toa_0", "toa_1", "toa_2")
+
+
+def gather_by_exchange(value, axis, dim):
+    size = lax.axis_size(axis)
+    repeats = [size if d == dim else 1 for d in range(value.ndim)]
+    return lax.all_to_all(
+        jnp.tile(value, repeats), axis, split_axis=dim, concat_axis=dim, tiled=True
+    )
 
 
 def in_blocks(value, dim, peers):
@@ -77,7 +85,7 @@
     weighted_res = (weight * residual).astype(jnp.bfloat16)
     tile_gram = jnp.einsum(
         "tkr,tjr->tkj",
-        lax.all_gather(basis_own, "rep", axis=1, tiled=True),
+        gather_by_exchange(basis_own, "rep", 1),
         scaled,
         preferred_element_type=jnp.float32,
     )

time: 155 us -> 133 us (0.86)
  waiting for transfers between devices: 73.1 us -> 51.5 us
  between operations: 14.3 us -> 0.95 us
  starting transfers between devices: 25.8 us -> 33.9 us
  local copies, waits for them, and re-layouts: 18.5 us -> 23.9 us
    all_gather x1 -> x0, waiting for transfers between devices: 21 us -> none  [pulsar_terms(): lax.all_gather(basis_own, 'rep', axis=1, tiled=True)]
    all_to_all x0 -> x1, starting transfers between devices: none -> 6.5 us  [gather_by_exchange(): lax.all_to_all(jnp.tile(value, repeats), axis, split_axis=dim, concat_axi...]
    another operation x0 -> x1, local copies, waits for them, and re-layouts: none -> 5.46 us  [gather_by_exchange(): jnp.tile(value, repeats)]
    convert_element_type x1, other arithmetic: 0.95 us -> 2.9 us  [pulsar_terms(): scaled = (weight[:, None, :] * basis_own).astype(jnp.bfloat16)]
  transfers between devices with their start and end apart: 4 -> 4, of which waited for: 4 -> 4; matrix products, arithmetic and copies ran while one was open for 9% -> 10% of each run, Pallas kernels for 0% -> 0%
where the time goes in v1:
time: 133 us
  waiting for transfers between devices  51.5 us (39%)
  starting transfers between devices  33.9 us (25%)
  local copies, waits for them, and re-layouts  23.9 us (18%)
  matrix products  17 us (13%)
  other arithmetic  5.46 us (4%)
    all_to_all x1, waiting for transfers between devices, sum_at_owner(): lax.all_to_all(in_blocks(value, dim, peers), axis, 0, 0, tiled=True)  32.1 us
    all_to_all x1, starting transfers between devices, sent_together(): lax.all_to_all(both, axis, split_axis=split_dim, concat_axis=concat_dim,...  16.4 us
    all_to_all x1, waiting for transfers between devices, sent_together(): lax.all_to_all(both, axis, split_axis=split_dim, concat_axis=concat_dim,...  11.6 us
    dot_general x1, matrix products, pulsar_terms(): jnp.einsum('tkr,tjr->tkj', gather_by_exchange(basis_own, 'rep', 1), scale...  10.3 us
    all_to_all x1, starting transfers between devices, sum_at_owner(): lax.all_to_all(in_blocks(value, dim, peers), axis, 0, 0, tiled=True)  7.61 us
    all_to_all x1, waiting for transfers between devices, summed_rows(): return jnp.sum(lax.all_to_all(own, far, 0, 0, tiled=True), axis=0)  7.56 us
    all_to_all x1, starting transfers between devices, gather_by_exchange(): lax.all_to_all(jnp.tile(value, repeats), axis, split_axis=dim, concat_axi...  6.5 us
    another operation x1, local copies, waits for them, and re-layouts, gather_by_exchange(): jnp.tile(value, repeats)  5.46 us
  transfers between devices with their start and end apart: 4, of which 4 were waited for; matrix products, arithmetic and copies ran while one was open for 10% of the time, Pallas kernels for 0%

profile of v1, /device:TPU:2, one launch (start us, length us, event | category | flops | bytes accessed | tf_op | source)
XLA Modules:
  0.0 132.8 jit_solution(13534905810883557754)
XLA Ops:
  0.6 5.5 %tile.4 = bf16[128,2,50,256]{3,0,2,1:T(8,128)(2,1)} broadcast(bf16[128,50,256]{2,0,1:T(8,128)(2,1)} %param.11), dimensions={0,2,3} | broadcast | bytes 9830400 | tf_op jit(solution)/shard_map/tile | solution.py:14
  6.1 6.5 %all-to-all-start = ((bf16[128,100,256]{2,0,1:T(8,128)(2,1)}), bf16[128,100,256]{2,0,1:T(8,128)(2,1)}, u32[]{:S(2)}, u32[]{:S(2)}) async-start(bf16[128,100,256]{2,0,1:T(8,128)(2,1)} %bitcast.27), calls=%async_computation | async-start | bytes 13107200 | tf_op jit(solution)/shard_map/all_to_all | solution.py:13
  13.5 2.9 %multiply_convert_fusion = bf16[128,50,256]{2,0,1:T(8,128)(2,1)S(1)} fusion(bf16[128,50,256]{2,0,1:T(8,128)(2,1)} %param.11, f32[128,256]{1,0:T(8,128)S(1)} %get-tuple-element.13), kind=kLoop, calls=%fused_computation.6 | loop fusion | flops 4915200 | bytes 6684672 | tf_op jit(solution)/shard_map/convert_element_type | solution.py:84
  16.4 1.9 %fusion.2 = f32[128,1,50]{2,1,0:T(1,128)S(1)} fusion(bf16[128,50,256]{2,0,1:T(8,128)(2,1)S(1)} %copy-done.1, bf16[128,256,1]{1,0,2:T(8,128)(2,1)S(1)} %fusion.15), kind=kOutput, calls=%fused_computation.7 | convolution fusion | flops 3276800 | bytes 3367936 | tf_op jit(solution)/shard_map/tjr,tr->tj/dot_general | solution.py:92
  18.8 10.3 %fusion.5 = f32[128,100,50]{1,2,0:T(8,128)} fusion(bf16[128,100,256]{2,0,1:T(8,128)(2,1)} %all-to-all-done, bf16[128,50,256]{2,0,1:T(8,128)(2,1)S(1)} %multiply_convert_fusion), kind=kOutput, calls=%fused_computation.11 | convolution fusion | flops 327680000 | bytes 12390400 | tf_op jit(solution)/shard_map/tkr,tjr->tkj/dot_general | solution.py:86
  29.1 3.7 %copy.31 = f32[128,100,50]{0,2,1:T(8,128)S(1)} copy(f32[128,100,50]{1,2,0:T(8,128)} %fusion.5) | data formatting | bytes 5120000 | tf_op jit(solution)/shard_map/tkr,tjr->tkj/dot_general | solution.py:86
  32.8 1.7 %reshape.42 = f32[128,5000]{0,1:T(8,128)} reshape(f32[128,100,50]{0,2,1:T(8,128)S(1)} %copy.31) | data formatting | bytes 5120000 | tf_op jit(solution)/shard_map/reshape | solution.py:99
  34.4 4.0 %fusion.19 = f32[128,5000]{0,1:T(8,128)S(1)} fusion(f32[128,5000]{0,1:T(8,128)} %reshape.42, s32[128]{0:T(128)S(1)} %copy-done.5), kind=kOutput, calls=%fused_computation.32 | convolution fusion | flops 983056384 | bytes 5120512 | tf_op jit(solution)/shard_map/dot_general | solution.py:97
  38.5 1.7 %pad_maximum_fusion = f32[128,5050]{0,1:T(8,128)} fusion(f32[128,50]{0,1:T(8,128)S(1)} %fusion.18, f32[128,5000]{0,1:T(8,128)S(1)} %fusion.19), kind=kLoop, calls=%fused_computation.10 | loop fusion | flops 646400 | bytes 5171200 | tf_op jit(solution)/shard_map/concatenate | solution.py:38
  40.1 2.1 %copy.32 = f32[128,5050]{1,0:T(8,128)S(1)} copy(f32[128,5050]{0,1:T(8,128)} %pad_maximum_fusion) | data formatting | bytes 5171200 | tf_op jit(solution)/shard_map/concatenate | solution.py:38
  42.3 3.0 %copy.33 = f32[16,8,1,5050]{3,1,2,0:T(8,128)} copy(f32[16,8,1,5050]{3,0,1,2:T(8,128)S(1)} %bitcast.28) | data formatting | bytes 5171200 | tf_op jit(solution)/shard_map/transpose | solution.py:21
  45.3 7.6 %all-to-all-start.1 = ((f32[16,8,1,5050]{3,1,2,0:T(8,128)}), f32[16,8,1,5050]{3,1,2,0:T(8,128)S(1)}, u32[]{:S(2)}, u32[]{:S(2)}) async-start(f32[16,8,1,5050]{3,1,2,0:T(8,128)} %copy.33), calls=%async_computation.1 | async-start | bytes 5242880 | tf_op jit(solution)/shard_map/all_to_all | solution.py:26
  53.4 1.0 scatter_custom_fusion
  54.4 1.2 gather_fusion.1
  55.8 0.8 gather_fusion
  56.5 0.9 copy.35
  57.4 32.1 %all-to-all-done.1 = f32[16,8,1,5050]{3,1,2,0:T(8,128)S(1)} async-done(((f32[16,8,1,5050]{3,1,2,0:T(8,128)}), f32[16,8,1,5050]{3,1,2,0:T(8,128)S(1)}, u32[]{:S(2)}, u32[]{:S(2)}) %all-to-all-start.1) | async-done | bytes 2585632 | tf_op jit(solution)/shard_map/all_to_all | solution.py:26
  89.5 16.4 %all-to-all-start.3 = ((f32[128,1,257]{2,1,0:T(1,128)}), f32[128,1,257]{2,1,0:T(1,128)S(1)}, u32[]{:S(2)}, u32[]{:S(2)}) async-start(f32[128,1,257]{2,1,0:T(1,128)} %copy.35), calls=%async_computation.3 | async-start | bytes 393216 | tf_op jit(solution)/shard_map/all_to_all | solution.py:55
  106.1 0.8 reduce_sum.52
  106.9 11.6 %all-to-all-done.3 = f32[128,1,257]{2,1,0:T(1,128)S(1)} async-done(((f32[128,1,257]{2,1,0:T(1,128)}), f32[128,1,257]{2,1,0:T(1,128)S(1)}, u32[]{:S(2)}, u32[]{:S(2)}) %all-to-all-start.3) | async-done | bytes 131616 | tf_op jit(solution)/shard_map/all_to_all | solution.py:55
  118.5 3.4 %all-to-all-start.2 = ((f32[8,1,5050]{2,1,0:T(1,128)}), f32[8,1,5050]{2,1,0:T(1,128)S(1)}, u32[]{:S(2)}, u32[]{:S(2)}) async-start(f32[8,1,5050]{2,1,0:T(1,128)} %reduce_sum.52), calls=%async_computation.2 | async-start | bytes 327680 | tf_op jit(solution)/shard_map/all_to_all | solution.py:33
  122.0 1.6 %scatter_custom_fusion.1 = f32[128,256]{1,0:T(8,128)} fusion(s32[128]{0:T(128)S(1)} %fusion.24, f32[128,257]{1,0:T(8,128)S(1)} %bitcast.29, f32[]{:T(128)} %constant.37.clone.1), kind=kCustom, calls=%fused_computation.18 | custom fusion | bytes 262148 | tf_op jit(solution)/shard_map/scatter | solution.py:133
  123.7 7.6 %all-to-all-done.2 = f32[8,1,5050]{2,1,0:T(1,128)S(1)} async-done(((f32[8,1,5050]{2,1,0:T(1,128)}), f32[8,1,5050]{2,1,0:T(1,128)S(1)}, u32[]{:S(2)}, u32[]{:S(2)}) %all-to-all-start.2) | async-done | bytes 161632 | tf_op jit(solution)/shard_map/all_to_all | solution.py:33
  132.1 0.7 copy.38
  (45 shorter events, 3.1 us)
Async XLA Ops:
  0.6 12.0 %copy-start = (f32[128,64]{0,1:T(8,128)S(1)}, f32[128,64]{0,1:T(8,128)}, u32[]{:S(2)}) copy-start(f32[128,64]{0,1:T(8,128)} %param.13) | copy-start | bytes 98308
  6.1 6.6 %copy-start.5 = (s32[128]{0:T(128)S(1)}, s32[128]{0:T(128)}, u32[]{:S(2)}) copy-start(s32[128]{0:T(128)} %param.14) | copy-start | bytes 1540
  6.1 6.6 %copy-start.7 = (s32[128]{0:T(128)S(1)}, s32[128]{0:T(128)}, u32[]{:S(2)}) copy-start(s32[128]{0:T(128)} %param.15) | copy-start | bytes 1540
  6.1 6.9 %copy-start.6 = (f32[128,64]{0,1:T(8,128)S(1)}, f32[128,64]{0,1:T(8,128)}, u32[]{:S(2)}) copy-start(f32[128,64]{0,1:T(8,128)} %param.12) | copy-start | bytes 98308
  6.1 7.2 %copy-start.2 = (f32[128,256]{1,0:T(8,128)S(1)}, f32[128,256]{1,0:T(8,128)}, u32[]{:S(2)}) copy-start(f32[128,256]{1,0:T(8,128)} %param.9) | copy-start | bytes 393220
  6.1 7.2 %copy-start.3 = (f32[128,256]{1,0:T(8,128)S(1)}, f32[128,256]{1,0:T(8,128)}, u32[]{:S(2)}) copy-start(f32[128,256]{1,0:T(8,128)} %param.10) | copy-start | bytes 393220
  6.1 7.2 %copy-start.4 = (s32[128]{0:T(128)S(1)}, s32[128]{0:T(128)}, u32[]{:S(2)}) copy-start(s32[128]{0:T(128)} %param.16) | copy-start | bytes 1540
  6.1 12.7 %all-to-all-start = ((bf16[128,100,256]{2,0,1:T(8,128)(2,1)}), bf16[128,100,256]{2,0,1:T(8,128)(2,1)}, u32[]{:S(2)}, u32[]{:S(2)}) async-start(bf16[128,100,256]{2,0,1:T(8,128)(2,1)} %bitcast.27), calls=%async_computation | async-start | bytes 13107200 | tf_op jit(solution)/shard_map/all_to_all | solution.py:13
  13.5 2.9 %copy-start.1 = (bf16[128,50,256]{2,0,1:T(8,128)(2,1)S(1)}, bf16[128,50,256]{2,0,1:T(8,128)(2,1)}, u32[]{:S(2)}) copy-start(bf16[128,50,256]{2,0,1:T(8,128)(2,1)} %param.11) | copy-start | bytes 9830404
  45.3 7.6 %copy-start.8 = (s32[128]{0:T(128)S(1)}, s32[128]{0:T(128)}, u32[]{:S(2)}) copy-start(s32[128]{0:T(128)} %param.17) | copy-start | bytes 1540
  45.3 44.2 %all-to-all-start.1 = ((f32[16,8,1,5050]{3,1,2,0:T(8,128)}), f32[16,8,1,5050]{3,1,2,0:T(8,128)S(1)}, u32[]{:S(2)}, u32[]{:S(2)}) async-start(f32[16,8,1,5050]{3,1,2,0:T(8,128)} %copy.33), calls=%async_computation.1 | async-start | bytes 5242880 | tf_op jit(solution)/shard_map/all_to_all | solution.py:26
  89.5 29.0 %all-to-all-start.3 = ((f32[128,1,257]{2,1,0:T(1,128)}), f32[128,1,257]{2,1,0:T(1,128)S(1)}, u32[]{:S(2)}, u32[]{:S(2)}) async-start(f32[128,1,257]{2,1,0:T(1,128)} %copy.35), calls=%async_computation.3 | async-start | bytes 393216 | tf_op jit(solution)/shard_map/all_to_all | solution.py:55
  118.5 12.7 %all-to-all-start.2 = ((f32[8,1,5050]{2,1,0:T(1,128)}), f32[8,1,5050]{2,1,0:T(1,128)S(1)}, u32[]{:S(2)}, u32[]{:S(2)}) async-start(f32[8,1,5050]{2,1,0:T(1,128)} %reduce_sum.52), calls=%async_computation.2 | async-start | bytes 327680 | tf_op jit(solution)/shard_map/all_to_all | solution.py:33
